TPU v7x, 32 devices: a whole 2x2x4 slice. The times are simulated.
32 devices in a mesh: groups: 2 (over y), gx: 4 (over z), gy: 4 (over x, core).
Axes of the slice: x: 2, y: 2, z: 4, core: 2. Of those that a mesh axis runs over, the one named last changes fastest.
Arguments:
- hidden_in: bfloat16 [128, 18432], P(('groups', 'gx'), 'gy'), parts along dimension 0, may hold values from -6 to 6
- w_query: bfloat16 [18432, 12288], P('gy', 'gx'), may hold values from -0.046875 to 0.046875
- w_out: bfloat16 [12288, 18432], P('gx', 'gy'), may hold values from -0.4375 to 0.4375
- cache_keys: bfloat16 [128, 1024, 256], P(('groups', 'gx', 'gy')), parts along dimension 0, may hold values from -250 to 250
- cache_values: bfloat16 [128, 1024, 256], P(('groups', 'gx', 'gy')), parts along dimension 0, may hold values from -6 to 6
- lengths: int32 [128], P(('groups', 'gx', 'gy')), parts along dimension 0, may hold values from 128 to 1024
Outputs:
- layer_out: bfloat16 [128, 18432], P(('groups', 'gx'), 'gy'), parts along dimension 0
There are 2 independent parts, one for each index of `groups`. A program takes and returns all parts, laid end to end along the dimension named above; an argument that names none is the same for every part. Nothing has to cross between parts.
All inputs are finite; a program needn't handle non-finite values.
Results may differ from a plain program's by a relative error of at most 0.0097.
Values may be sent and summed in bfloat16 or wider, within the bound.
No kernel may reach another device: no remote copies, remote signals or barrier semaphores. Data moves between devices by JAX's collectives and lax.ppermute only.
A program may use at most 128 MiB of HBM per device.

v0:
```python
import jax
import jax.numpy as jnp
from jax import lax
from jax.experimental import pallas as pl
from jax.experimental.pallas import tpu as pltpu
from jax.sharding import PartitionSpec as P

NEAR = 8


def shift(x, axis, step):
    size = lax.axis_size(axis)
    return lax.ppermute(x, axis, [(i, (i + step) % size) for i in range(size)])


def near(axis):
    return lax.axis_size(axis) <= NEAR


def gather(x, axis):
    if not near(axis):
        return lax.all_gather(x, axis, axis=0)
    return jnp.stack([x] + [shift(x, axis, s) for s in range(1, lax.axis_size(axis))])


def swap(x, axis, sign):
    if not near(axis):
        return lax.all_to_all(x, axis, split_axis=0, concat_axis=0)
    return jnp.stack([x[0]] + [shift(x[s], axis, sign * s) for s in range(1, lax.axis_size(axis))])


def reduce_back(x, axis, sent):
    if not near(axis):
        return lax.psum_scatter(x, axis, scatter_dimension=0)
    total = x[0]
    for piece in [shift(x[s].astype(sent), axis, -s) for s in range(1, lax.axis_size(axis))]:
        total = total + piece.astype(jnp.float32)
    return total


def by_source(x, axis):
    if not near(axis):
        return x
    size = lax.axis_size(axis)
    doubled = jnp.concatenate([x[::-1], x[::-1]])
    return lax.dynamic_slice_in_dim(doubled, size - 1 - lax.axis_index(axis), size, 0)


def reduce_to(x, axis):
    if not near(axis):
        return lax.psum_scatter(x, axis, scatter_dimension=0)
    size = lax.axis_size(axis)
    me = lax.axis_index(axis)
    pick = lambda dst: lax.dynamic_index_in_dim(x, dst, 0, keepdims=False)
    total = pick(me)
    for piece in [shift(pick((me + s) % size), axis, s) for s in range(1, size)]:
        total = total + piece
    return total


def parts(width, count):
    count = count if width % (count * 128) == 0 else 1
    return [(i * (width // count), (i + 1) * (width // count)) for i in range(count)]


def product(x, w, k, n, base=None):
    rows, depth = x.shape
    width = n[1] - n[0]
    tile = next(t for t in (512, 384, 256, 128) if width % t == 0 and n[0] % t == 0)
    first = n[0] // tile
    row = k[0] // depth

    def kernel(x_ref, w_ref, *rest):
        acc = jnp.dot(x_ref[...], w_ref[...], preferred_element_type=jnp.float32)
        rest[-1][...] = acc if base is None else acc + rest[0][...]

    in_specs = [
        pl.BlockSpec((rows, depth), lambda j: (0, 0)),
        pl.BlockSpec((depth, tile), lambda j: (row, first + j)),
    ]
    if base is not None:
        in_specs.append(pl.BlockSpec((rows, tile), lambda j: (0, first + j)))
    return pl.pallas_call(
        kernel,
        grid=(width // tile,),
        in_specs=in_specs,
        out_specs=pl.BlockSpec((rows, tile), lambda j: (0, j)),
        out_shape=jax.ShapeDtypeStruct((rows, width), jnp.float32),
        compiler_params=pltpu.CompilerParams(vmem_limit_bytes=40 * 2**20),
    )(x, w, *(() if base is None else (base,)))


def step(hidden_in, w_query, w_out, cache_keys, cache_values, lengths):
    across = lax.axis_size("gx")
    within = lax.axis_size("gy")
    local_seqs, slot_count, head_dim = cache_keys.shape
    rows = across * within * local_seqs
    slice_width = w_query.shape[1]

    k0, k1 = parts(hidden_in.shape[1], 2)
    x0 = gather(hidden_in[:, k0[0]:k0[1]], "gx").reshape(rows, -1)
    x1 = gather(hidden_in[:, k1[0]:k1[1]], "gx").reshape(rows, -1)
    base = product(x0, w_query, k0, (0, slice_width))
    owned = []
    for n in parts(slice_width, 2):
        part = product(x1, w_query, k1, n, base)
        part = part.reshape(across, within, local_seqs, -1).transpose(1, 0, 2, 3)
        owned.append(reduce_to(part, "gy").astype(jnp.bfloat16))
    owned = jnp.concatenate(owned, axis=2)
    query = swap(owned, "gx", -1).transpose(1, 0, 2).reshape(local_seqs, -1)

    head_count = query.shape[1] // head_dim
    query_heads = query.reshape(local_seqs, head_count, head_dim)
    scores = jnp.einsum("bhd,bld->bhl", query_heads, cache_keys, preferred_element_type=jnp.float32)
    scores = scores / jnp.sqrt(jnp.float32(head_dim))
    live_slots = jnp.arange(slot_count)[None, None, :] < lengths[:, None, None]
    scores = jnp.where(live_slots, scores, jnp.float32(-1e30))
    top_score = jnp.max(scores, axis=2, keepdims=True)
    expo = jnp.where(live_slots, jnp.exp(scores - top_score), jnp.float32(0.0))
    probs = (expo / jnp.sum(expo, axis=2, keepdims=True)).astype(jnp.bfloat16)
    mixed = jnp.einsum("bhl,bld->bhd", probs, cache_values, preferred_element_type=jnp.float32)
    attended = mixed.astype(jnp.bfloat16).reshape(local_seqs, across, slice_width)

    spread = swap(attended.transpose(1, 0, 2), "gx", 1)
    head_rows = gather(spread, "gy").transpose(1, 0, 2, 3).reshape(rows, slice_width)
    outs = []
    for n in parts(w_out.shape[1], 3):
        part = product(head_rows, w_out, (0, slice_width), n)
        part = part.reshape(across, within * local_seqs, -1)
        outs.append(reduce_back(part, "gx", jnp.bfloat16).astype(jnp.bfloat16))
    out = jnp.concatenate(outs, axis=1).reshape(within, local_seqs, -1)
    return by_source(out, "gy").reshape(within * local_seqs, -1)


def solution(mesh):
    placed = (
        P(("groups", "gx"), "gy"),
        P("gy", "gx"),
        P("gx", "gy"),
        P(("groups", "gx", "gy"), None, None),
        P(("groups", "gx", "gy"), None, None),
        P(("groups", "gx", "gy")),
    )
    return jax.shard_map(
        step, mesh=mesh, in_specs=placed, out_specs=P(("groups", "gx"), "gy"), check_vma=False
    )
```

profile of v0, /device:TPU:0, one launch (start us, length us, event | category | flops | bytes accessed | tf_op | source)
XLA Modules:
  0.0 103.1 jit_solution(2529375033148127628)
XLA Ops:
  0.0 1.1 %slice_bitcast_fusion.3 = (bf16[1,16,2304]{2,1,0:T(8,128)(2,1)S(1)}, bf16[1,16,2304]{2,1,0:T(8,128)(2,1)S(1)}, bf16[16,2304]{1,0:T(8,128)(2,1)S(1)}, bf16[16,2304]{1,0:T(8,128)(2,1)S(1)}) fusion(bf16[16,4608]{1,0:T(8,128)(2,1)} %param.6), kind=kLoop, calls=%fused_computation.64 | loop fusion | bytes 442368 | tf_op jit(solution)/shard_map/stack | solution.py:23
  1.1 4.1 %collective-permute-start.4 = (bf16[16,2304]{1,0:T(8,128)(2,1)S(1)}, bf16[16,2304]{1,0:T(8,128)(2,1)S(1)}, u32[]{:S(2)}, u32[]{:S(2)}) collective-permute-start(bf16[16,2304]{1,0:T(8,128)(2,1)S(1)} %get-tuple-element.22), channel_id=1, source_target_pairs={{0,8},{4,12},{8,0},{12,4},{1,9},{5,13},{9,1},{13,5},{2,10},{6,14},... | collective-permute-start | bytes 221192 | tf_op jit(solution)/shard_map/ppermute | solution.py:13
  5.2 1.6 %collective-permute-start.3 = (bf16[16,2304]{1,0:T(8,128)(2,1)S(1)}, bf16[16,2304]{1,0:T(8,128)(2,1)S(1)}, u32[]{:S(2)}, u32[]{:S(2)}) collective-permute-start(bf16[16,2304]{1,0:T(8,128)(2,1)S(1)} %get-tuple-element.22), channel_id=1, source_target_pairs={{0,4},{4,8},{8,12},{12,0},{1,5},{5,9},{9,13},{13,1},{2,6},{6,10},{... | collective-permute-start | bytes 221192 | tf_op jit(solution)/shard_map/ppermute | solution.py:13
  6.8 2.2 %collective-permute-start.5 = (bf16[16,2304]{1,0:T(8,128)(2,1)S(1)}, bf16[16,2304]{1,0:T(8,128)(2,1)S(1)}, u32[]{:S(2)}, u32[]{:S(2)}) collective-permute-start(bf16[16,2304]{1,0:T(8,128)(2,1)S(1)} %get-tuple-element.22), channel_id=1, source_target_pairs={{0,12},{4,0},{8,4},{12,8},{1,13},{5,1},{9,5},{13,9},{2,14},{6,2},{... | collective-permute-start | bytes 221192 | tf_op jit(solution)/shard_map/ppermute | solution.py:13
  9.1 0.6 collective-permute-start
  9.6 0.6 collective-permute-done.4
  10.2 3.0 %collective-permute-start.2 = (bf16[16,2304]{1,0:T(8,128)(2,1)S(1)}, bf16[16,2304]{1,0:T(8,128)(2,1)S(1)}, u32[]{:S(2)}, u32[]{:S(2)}) collective-permute-start(bf16[16,2304]{1,0:T(8,128)(2,1)S(1)} %get-tuple-element.23), channel_id=1, source_target_pairs={{0,12},{4,0},{8,4},{12,8},{1,13},{5,1},{9,5},{13,9},{2,14},{6,2},{... | collective-permute-start | bytes 221192 | tf_op jit(solution)/shard_map/ppermute | solution.py:13
  13.2 7.7 %shard_map.64.rest_0_ = f32[64,3072]{1,0:T(8,128)S(1)} custom-call(bf16[64,2304]{1,0:T(8,128)(2,1)S(1)} %bitcast.83, bf16[4608,3072]{1,0:T(8,128)(2,1)} %w_ref.8), custom_call_target="tpu_custom_call" | custom-call | tf_op jit(solution)/shard_map/pallas_call | solution.py:83
  21.0 4.5 %shard_map.66 = f32[64,1536]{1,0:T(8,128)S(1)} custom-call(bf16[64,2304]{1,0:T(8,128)(2,1)S(1)} %bitcast.81, bf16[4608,3072]{1,0:T(8,128)(2,1)} %w_ref.8, f32[64,3072]{1,0:T(8,128)S(1)} %shard_map.64.rest_0_), custom_call_target="tpu_custom_call" | custom-call | tf_op jit(solution)/shard_map/pallas_call | solution.py:83
  25.5 4.5 %shard_map.65 = f32[64,1536]{1,0:T(8,128)S(1)} custom-call(bf16[64,2304]{1,0:T(8,128)(2,1)S(1)} %bitcast.82, bf16[4608,3072]{1,0:T(8,128)(2,1)} %w_ref.8, f32[64,3072]{1,0:T(8,128)S(1)} %shard_map.64.rest_0_), custom_call_target="tpu_custom_call" | custom-call | tf_op jit(solution)/shard_map/pallas_call | solution.py:83
  30.4 1.7 %collective-permute-start.11 = (f32[4,4,1536]{2,1,0:T(4,128)S(1)}, f32[4,4,1536]{2,1,0:T(4,128)S(1)}, u32[]{:S(2)}, u32[]{:S(2)}) collective-permute-start(f32[4,4,1536]{2,1,0:T(4,128)S(1)} %get-tuple-element.9), channel_id=1, source_target_pairs={{0,3},{1,0},{2,1},{3,2},{4,7},{5,4},{6,5},{7,6},{8,11},{9,8},{10,9... | collective-permute-start | bytes 294920 | tf_op jit(solution)/shard_map/ppermute | solution.py:13
  32.1 1.5 %collective-permute-start.10 = (f32[4,4,1536]{2,1,0:T(4,128)S(1)}, f32[4,4,1536]{2,1,0:T(4,128)S(1)}, u32[]{:S(2)}, u32[]{:S(2)}) collective-permute-start(f32[4,4,1536]{2,1,0:T(4,128)S(1)} %get-tuple-element.10), channel_id=1, source_target_pairs={{0,2},{1,3},{2,0},{3,1},{4,6},{5,7},{6,4},{7,5},{8,10},{9,11},{10,... | collective-permute-start | bytes 294920 | tf_op jit(solution)/shard_map/ppermute | solution.py:13
  33.7 1.7 %collective-permute-start.8 = (f32[4,4,1536]{2,1,0:T(4,128)S(1)}, f32[4,4,1536]{2,1,0:T(4,128)S(1)}, u32[]{:S(2)}, u32[]{:S(2)}) collective-permute-start(f32[4,4,1536]{2,1,0:T(4,128)S(1)} %get-tuple-element.6), channel_id=1, source_target_pairs={{0,3},{1,0},{2,1},{3,2},{4,7},{5,4},{6,5},{7,6},{8,11},{9,8},{10,9... | collective-permute-start | bytes 294920 | tf_op jit(solution)/shard_map/ppermute | solution.py:13
  35.4 0.7 collective-permute-start.7
  36.1 2.7 %collective-permute-done.10 = f32[4,4,1536]{2,1,0:T(4,128)S(1)} collective-permute-done((f32[4,4,1536]{2,1,0:T(4,128)S(1)}, f32[4,4,1536]{2,1,0:T(4,128)S(1)}, u32[]{:S(2)}, u32[]{:S(2)}) %collective-permute-start.10) | collective-permute-done | bytes 98336 | tf_op jit(solution)/shard_map/ppermute | solution.py:13
  38.8 0.7 collective-permute-done.8
  39.5 2.4 %collective-permute-done.7 = f32[4,4,1536]{2,1,0:T(4,128)S(1)} collective-permute-done((f32[4,4,1536]{2,1,0:T(4,128)S(1)}, f32[4,4,1536]{2,1,0:T(4,128)S(1)}, u32[]{:S(2)}, u32[]{:S(2)}) %collective-permute-start.7) | collective-permute-done | bytes 98336 | tf_op jit(solution)/shard_map/ppermute | solution.py:13
  42.0 2.9 %collective-permute-start.12 = (bf16[4,3072]{1,0:T(4,128)(2,1)S(1)}, bf16[4,3072]{1,0:T(4,128)(2,1)S(1)}, u32[]{:S(2)}, u32[]{:S(2)}) collective-permute-start(bf16[4,3072]{1,0:T(4,128)(2,1)S(1)} %get-tuple-element.29), channel_id=1, source_target_pairs={{0,12},{4,0},{8,4},{12,8},{1,13},{5,1},{9,5},{13,9},{2,14},{6,2},{... | collective-permute-start | bytes 73736 | tf_op jit(solution)/shard_map/ppermute | solution.py:13
  44.9 3.6 %collective-permute-start.13 = (bf16[4,3072]{1,0:T(4,128)(2,1)S(1)}, bf16[4,3072]{1,0:T(4,128)(2,1)S(1)}, u32[]{:S(2)}, u32[]{:S(2)}) collective-permute-start(bf16[4,3072]{1,0:T(4,128)(2,1)S(1)} %get-tuple-element.31), channel_id=1, source_target_pairs={{0,8},{4,12},{8,0},{12,4},{1,9},{5,13},{9,1},{13,5},{2,10},{6,14},... | collective-permute-start | bytes 73736 | tf_op jit(solution)/shard_map/ppermute | solution.py:13
  48.6 2.0 %collective-permute-done.14 = bf16[4,3072]{1,0:T(4,128)(2,1)S(1)} collective-permute-done((bf16[4,3072]{1,0:T(4,128)(2,1)S(1)}, bf16[4,3072]{1,0:T(4,128)(2,1)S(1)}, u32[]{:S(2)}, u32[]{:S(2)}) %collective-permute-start.14) | collective-permute-done | bytes 24608 | tf_op jit(solution)/shard_map/ppermute | solution.py:13
  50.8 0.7 fusion.4
  51.5 0.3 fusion.34
  51.9 2.1 %convolution_convert_fusion = bf16[4,48,256]{2,1,0:T(8,128)(2,1)S(1)} fusion(bf16[4,1024,256]{2,1,0:T(8,128)(2,1)} %param.10, f32[4,48]{1,0:T(4,128)S(1)} %fusion.34, f32[4,48,1024]{2,1,0:T(8,128)S(1)} %fusion.4, pred[4,1024]{1,0:T(4,128)(4,1)S(1)} %iota_compare_fusion), kind=kOutput, calls=%fused_computation.6 | convolution fusion | flops 101500096 | bytes 2986752 | tf_op jit(solution)/shard_map/bhl,bld->bhd/dot_general | solution.py:121
  54.1 2.9 %collective-permute-start.17 = (bf16[4,3072]{1,0:T(4,128)(2,1)S(1)}, bf16[4,3072]{1,0:T(4,128)(2,1)S(1)}, u32[]{:S(2)}, u32[]{:S(2)}) collective-permute-start(bf16[4,3072]{1,0:T(4,128)(2,1)S(1)} %get-tuple-element.25), channel_id=1, source_target_pairs={{0,12},{4,0},{8,4},{12,8},{1,13},{5,1},{9,5},{13,9},{2,14},{6,2},{... | collective-permute-start | bytes 73736 | tf_op jit(solution)/shard_map/ppermute | solution.py:13
  57.0 1.8 %collective-permute-start.15 = (bf16[4,3072]{1,0:T(4,128)(2,1)S(1)}, bf16[4,3072]{1,0:T(4,128)(2,1)S(1)}, u32[]{:S(2)}, u32[]{:S(2)}) collective-permute-start(bf16[4,3072]{1,0:T(4,128)(2,1)S(1)} %get-tuple-element.27), channel_id=1, source_target_pairs={{0,4},{4,8},{8,12},{12,0},{1,5},{5,9},{9,13},{13,1},{2,6},{6,10},{... | collective-permute-start | bytes 73736 | tf_op jit(solution)/shard_map/ppermute | solution.py:13
  58.9 2.9 %collective-permute-done.16 = bf16[4,3072]{1,0:T(4,128)(2,1)S(1)} collective-permute-done((bf16[4,3072]{1,0:T(4,128)(2,1)S(1)}, bf16[4,3072]{1,0:T(4,128)(2,1)S(1)}, u32[]{:S(2)}, u32[]{:S(2)}) %collective-permute-start.16) | collective-permute-done | bytes 24608 | tf_op jit(solution)/shard_map/ppermute | solution.py:13
  61.8 0.9 collective-permute-done.15
  62.8 1.4 %collective-permute-start.19 = (bf16[4,4,3072]{2,1,0:T(4,128)(2,1)S(1)}, bf16[4,4,3072]{2,1,0:T(4,128)(2,1)S(1)}, u32[]{:S(2)}, u32[]{:S(2)}) collective-permute-start(bf16[4,4,3072]{2,1,0:T(4,128)(2,1)S(1)} %pad_maximum_fusion.3), channel_id=1, source_target_pairs={{0,2},{1,3},{2,0},{3,1},{4,6},{5,7},{6,4},{7,5},{8,10},{9,11},{10,... | collective-permute-start | bytes 294920 | tf_op jit(solution)/shard_map/ppermute | solution.py:13
  64.2 1.7 %collective-permute-start.20 = (bf16[4,4,3072]{2,1,0:T(4,128)(2,1)S(1)}, bf16[4,4,3072]{2,1,0:T(4,128)(2,1)S(1)}, u32[]{:S(2)}, u32[]{:S(2)}) collective-permute-start(bf16[4,4,3072]{2,1,0:T(4,128)(2,1)S(1)} %pad_maximum_fusion.3), channel_id=1, source_target_pairs={{0,3},{1,0},{2,1},{3,2},{4,7},{5,4},{6,5},{7,6},{8,11},{9,8},{10,9... | collective-permute-start | bytes 294920 | tf_op jit(solution)/shard_map/ppermute | solution.py:13
  66.0 1.8 %collective-permute-done.19 = bf16[4,4,3072]{2,1,0:T(4,128)(2,1)S(1)} collective-permute-done((bf16[4,4,3072]{2,1,0:T(4,128)(2,1)S(1)}, bf16[4,4,3072]{2,1,0:T(4,128)(2,1)S(1)}, u32[]{:S(2)}, u32[]{:S(2)}) %collective-permute-start.19) | collective-permute-done | bytes 98336 | tf_op jit(solution)/shard_map/ppermute | solution.py:13
  67.7 1.1 %collective-permute-done.18 = bf16[4,4,3072]{2,1,0:T(4,128)(2,1)S(1)} collective-permute-done((bf16[4,4,3072]{2,1,0:T(4,128)(2,1)S(1)}, bf16[4,4,3072]{2,1,0:T(4,128)(2,1)S(1)}, u32[]{:S(2)}, u32[]{:S(2)}) %collective-permute-start.18) | collective-permute-done | bytes 98336 | tf_op jit(solution)/shard_map/ppermute | solution.py:13
  68.9 0.3 maximum_bitcast_fusion
  69.3 5.2 %shard_map.69 = f32[64,1536]{1,0:T(8,128)S(1)} custom-call(bf16[64,3072]{1,0:T(8,128)(2,1)S(1)} %reshape.95.x_ref, bf16[3072,4608]{1,0:T(8,128)(2,1)} %w_ref.11), custom_call_target="tpu_custom_call" | custom-call | tf_op jit(solution)/shard_map/pallas_call | solution.py:83
  74.5 5.2 %shard_map.68 = f32[64,1536]{1,0:T(8,128)S(1)} custom-call(bf16[64,3072]{1,0:T(8,128)(2,1)S(1)} %reshape.95.x_ref, bf16[3072,4608]{1,0:T(8,128)(2,1)} %w_ref.11), custom_call_target="tpu_custom_call" | custom-call | tf_op jit(solution)/shard_map/pallas_call | solution.py:83
  79.7 5.2 %shard_map.67 = f32[64,1536]{1,0:T(8,128)S(1)} custom-call(bf16[64,3072]{1,0:T(8,128)(2,1)S(1)} %reshape.95.x_ref, bf16[3072,4608]{1,0:T(8,128)(2,1)} %w_ref.11), custom_call_target="tpu_custom_call" | custom-call | tf_op jit(solution)/shard_map/pallas_call | solution.py:83
  85.0 0.8 collective-permute-start.27
  85.9 1.2 %collective-permute-start.29 = (bf16[16,1536]{1,0:T(8,128)(2,1)S(1)}, bf16[16,1536]{1,0:T(8,128)(2,1)S(1)}, u32[]{:S(2)}, u32[]{:S(2)}) collective-permute-start(bf16[16,1536]{1,0:T(8,128)(2,1)S(1)} %get-tuple-element.18), channel_id=1, source_target_pairs={{0,4},{4,8},{8,12},{12,0},{1,5},{5,9},{9,13},{13,1},{2,6},{6,10},{... | collective-permute-start | bytes 147464 | tf_op jit(solution)/shard_map/ppermute | solution.py:13
  87.1 1.1 %collective-permute-start.28 = (bf16[16,1536]{1,0:T(8,128)(2,1)S(1)}, bf16[16,1536]{1,0:T(8,128)(2,1)S(1)}, u32[]{:S(2)}, u32[]{:S(2)}) collective-permute-start(bf16[16,1536]{1,0:T(8,128)(2,1)S(1)} %get-tuple-element.19), channel_id=1, source_target_pairs={{0,8},{4,12},{8,0},{12,4},{1,9},{5,13},{9,1},{13,5},{2,10},{6,14},... | collective-permute-start | bytes 147464 | tf_op jit(solution)/shard_map/ppermute | solution.py:13
  88.3 1.5 %collective-permute-start.21 = (bf16[16,1536]{1,0:T(8,128)(2,1)S(1)}, bf16[16,1536]{1,0:T(8,128)(2,1)S(1)}, u32[]{:S(2)}, u32[]{:S(2)}) collective-permute-start(bf16[16,1536]{1,0:T(8,128)(2,1)S(1)} %get-tuple-element.11), channel_id=1, source_target_pairs={{0,12},{4,0},{8,4},{12,8},{1,13},{5,1},{9,5},{13,9},{2,14},{6,2},{... | collective-permute-start | bytes 147464 | tf_op jit(solution)/shard_map/ppermute | solution.py:13
  89.8 0.6 collective-permute-start.23
  90.5 1.8 %collective-permute-start.22 = (bf16[16,1536]{1,0:T(8,128)(2,1)S(1)}, bf16[16,1536]{1,0:T(8,128)(2,1)S(1)}, u32[]{:S(2)}, u32[]{:S(2)}) collective-permute-start(bf16[16,1536]{1,0:T(8,128)(2,1)S(1)} %get-tuple-element.13), channel_id=1, source_target_pairs={{0,8},{4,12},{8,0},{12,4},{1,9},{5,13},{9,1},{13,5},{2,10},{6,14},... | collective-permute-start | bytes 147464 | tf_op jit(solution)/shard_map/ppermute | solution.py:13
  92.3 2.6 %collective-permute-start.24 = (bf16[16,1536]{1,0:T(8,128)(2,1)S(1)}, bf16[16,1536]{1,0:T(8,128)(2,1)S(1)}, u32[]{:S(2)}, u32[]{:S(2)}) collective-permute-start(bf16[16,1536]{1,0:T(8,128)(2,1)S(1)} %get-tuple-element.14), channel_id=1, source_target_pairs={{0,12},{4,0},{8,4},{12,8},{1,13},{5,1},{9,5},{13,9},{2,14},{6,2},{... | collective-permute-start | bytes 147464 | tf_op jit(solution)/shard_map/ppermute | solution.py:13
  94.9 2.5 %collective-permute-start.25 = (bf16[16,1536]{1,0:T(8,128)(2,1)S(1)}, bf16[16,1536]{1,0:T(8,128)(2,1)S(1)}, u32[]{:S(2)}, u32[]{:S(2)}) collective-permute-start(bf16[16,1536]{1,0:T(8,128)(2,1)S(1)} %get-tuple-element.16), channel_id=1, source_target_pairs={{0,8},{4,12},{8,0},{12,4},{1,9},{5,13},{9,1},{13,5},{2,10},{6,14},... | collective-permute-start | bytes 147464 | tf_op jit(solution)/shard_map/ppermute | solution.py:13
  97.4 0.6 collective-permute-done.22
  98.0 3.0 %collective-permute-done.26 = bf16[16,1536]{1,0:T(8,128)(2,1)S(1)} collective-permute-done((bf16[16,1536]{1,0:T(8,128)(2,1)S(1)}, bf16[16,1536]{1,0:T(8,128)(2,1)S(1)}, u32[]{:S(2)}, u32[]{:S(2)}) %collective-permute-start.26) | collective-permute-done | bytes 49184 | tf_op jit(solution)/shard_map/ppermute | solution.py:13
  100.9 1.1 %collective-permute-done.25 = bf16[16,1536]{1,0:T(8,128)(2,1)S(1)} collective-permute-done((bf16[16,1536]{1,0:T(8,128)(2,1)S(1)}, bf16[16,1536]{1,0:T(8,128)(2,1)S(1)}, u32[]{:S(2)}, u32[]{:S(2)}) %collective-permute-start.25) | collective-permute-done | bytes 49184 | tf_op jit(solution)/shard_map/ppermute | solution.py:13
  102.2 0.2 fusion.6
  102.4 0.7 reshape.97
  (62 shorter events, 1.6 us)
Async XLA Ops:
  0.0 50.8 %copy-start = (bf16[4,1024,256]{2,1,0:T(8,128)(2,1)S(1)}, bf16[4,1024,256]{2,1,0:T(8,128)(2,1)}, u32[]{:S(2)}) copy-start(bf16[4,1024,256]{2,1,0:T(8,128)(2,1)} %param.9) | copy-start | bytes 6291460
  1.1 9.1 %collective-permute-start.4 = (bf16[16,2304]{1,0:T(8,128)(2,1)S(1)}, bf16[16,2304]{1,0:T(8,128)(2,1)S(1)}, u32[]{:S(2)}, u32[]{:S(2)}) collective-permute-start(bf16[16,2304]{1,0:T(8,128)(2,1)S(1)} %get-tuple-element.22), channel_id=1, source_target_pairs={{0,8},{4,12},{8,0},{12,4},{1,9},{5,13},{9,1},{13,5},{2,10},{6,14},... | collective-permute-start | bytes 221192 | tf_op jit(solution)/shard_map/ppermute | solution.py:13
  5.2 8.0 %collective-permute-start.3 = (bf16[16,2304]{1,0:T(8,128)(2,1)S(1)}, bf16[16,2304]{1,0:T(8,128)(2,1)S(1)}, u32[]{:S(2)}, u32[]{:S(2)}) collective-permute-start(bf16[16,2304]{1,0:T(8,128)(2,1)S(1)} %get-tuple-element.22), channel_id=1, source_target_pairs={{0,4},{4,8},{8,12},{12,0},{1,5},{5,9},{9,13},{13,1},{2,6},{6,10},{... | collective-permute-start | bytes 221192 | tf_op jit(solution)/shard_map/ppermute | solution.py:13
  6.8 6.4 %collective-permute-start.5 = (bf16[16,2304]{1,0:T(8,128)(2,1)S(1)}, bf16[16,2304]{1,0:T(8,128)(2,1)S(1)}, u32[]{:S(2)}, u32[]{:S(2)}) collective-permute-start(bf16[16,2304]{1,0:T(8,128)(2,1)S(1)} %get-tuple-element.22), channel_id=1, source_target_pairs={{0,12},{4,0},{8,4},{12,8},{1,13},{5,1},{9,5},{13,9},{2,14},{6,2},{... | collective-permute-start | bytes 221192 | tf_op jit(solution)/shard_map/ppermute | solution.py:13
  9.1 11.9 %collective-permute-start.1 = (bf16[16,2304]{1,0:T(8,128)(2,1)S(1)}, bf16[16,2304]{1,0:T(8,128)(2,1)S(1)}, u32[]{:S(2)}, u32[]{:S(2)}) collective-permute-start(bf16[16,2304]{1,0:T(8,128)(2,1)S(1)} %get-tuple-element.23), channel_id=1, source_target_pairs={{0,8},{4,12},{8,0},{12,4},{1,9},{5,13},{9,1},{13,5},{2,10},{6,14},... | collective-permute-start | bytes 221192 | tf_op jit(solution)/shard_map/ppermute | solution.py:13
  9.1 11.9 %collective-permute-start = (bf16[16,2304]{1,0:T(8,128)(2,1)S(1)}, bf16[16,2304]{1,0:T(8,128)(2,1)S(1)}, u32[]{:S(2)}, u32[]{:S(2)}) collective-permute-start(bf16[16,2304]{1,0:T(8,128)(2,1)S(1)} %get-tuple-element.23), channel_id=1, source_target_pairs={{0,4},{4,8},{8,12},{12,0},{1,5},{5,9},{9,13},{13,1},{2,6},{6,10},{... | collective-permute-start | bytes 221192 | tf_op jit(solution)/shard_map/ppermute | solution.py:13
  10.2 10.8 %collective-permute-start.2 = (bf16[16,2304]{1,0:T(8,128)(2,1)S(1)}, bf16[16,2304]{1,0:T(8,128)(2,1)S(1)}, u32[]{:S(2)}, u32[]{:S(2)}) collective-permute-start(bf16[16,2304]{1,0:T(8,128)(2,1)S(1)} %get-tuple-element.23), channel_id=1, source_target_pairs={{0,12},{4,0},{8,4},{12,8},{1,13},{5,1},{9,5},{13,9},{2,14},{6,2},{... | collective-permute-start | bytes 221192 | tf_op jit(solution)/shard_map/ppermute | solution.py:13
  30.0 18.5 %copy-start.2 = (s32[4]{0:T(128)S(1)}, s32[4]{0:T(128)}, u32[]{:S(2)}) copy-start(s32[4]{0:T(128)} %param.11) | copy-start | bytes 52
  30.3 5.1 %collective-permute-start.9 = (f32[4,4,1536]{2,1,0:T(4,128)S(1)}, f32[4,4,1536]{2,1,0:T(4,128)S(1)}, u32[]{:S(2)}, u32[]{:S(2)}) collective-permute-start(f32[4,4,1536]{2,1,0:T(4,128)S(1)} %get-tuple-element.8), channel_id=1, source_target_pairs={{0,1},{1,2},{2,3},{3,0},{4,5},{5,6},{6,7},{7,4},{8,9},{9,10},{10,1... | collective-permute-start | bytes 294920 | tf_op jit(solution)/shard_map/ppermute | solution.py:13
  30.4 5.8 %collective-permute-start.11 = (f32[4,4,1536]{2,1,0:T(4,128)S(1)}, f32[4,4,1536]{2,1,0:T(4,128)S(1)}, u32[]{:S(2)}, u32[]{:S(2)}) collective-permute-start(f32[4,4,1536]{2,1,0:T(4,128)S(1)} %get-tuple-element.9), channel_id=1, source_target_pairs={{0,3},{1,0},{2,1},{3,2},{4,7},{5,4},{6,5},{7,6},{8,11},{9,8},{10,9... | collective-permute-start | bytes 294920 | tf_op jit(solution)/shard_map/ppermute | solution.py:13
  32.1 6.7 %collective-permute-start.10 = (f32[4,4,1536]{2,1,0:T(4,128)S(1)}, f32[4,4,1536]{2,1,0:T(4,128)S(1)}, u32[]{:S(2)}, u32[]{:S(2)}) collective-permute-start(f32[4,4,1536]{2,1,0:T(4,128)S(1)} %get-tuple-element.10), channel_id=1, source_target_pairs={{0,2},{1,3},{2,0},{3,1},{4,6},{5,7},{6,4},{7,5},{8,10},{9,11},{10,... | collective-permute-start | bytes 294920 | tf_op jit(solution)/shard_map/ppermute | solution.py:13
  33.6 5.2 %collective-permute-start.6 = (f32[4,4,1536]{2,1,0:T(4,128)S(1)}, f32[4,4,1536]{2,1,0:T(4,128)S(1)}, u32[]{:S(2)}, u32[]{:S(2)}) collective-permute-start(f32[4,4,1536]{2,1,0:T(4,128)S(1)} %get-tuple-element.5), channel_id=1, source_target_pairs={{0,1},{1,2},{2,3},{3,0},{4,5},{5,6},{6,7},{7,4},{8,9},{9,10},{10,1... | collective-permute-start | bytes 294920 | tf_op jit(solution)/shard_map/ppermute | solution.py:13
  33.7 5.8 %collective-permute-start.8 = (f32[4,4,1536]{2,1,0:T(4,128)S(1)}, f32[4,4,1536]{2,1,0:T(4,128)S(1)}, u32[]{:S(2)}, u32[]{:S(2)}) collective-permute-start(f32[4,4,1536]{2,1,0:T(4,128)S(1)} %get-tuple-element.6), channel_id=1, source_target_pairs={{0,3},{1,0},{2,1},{3,2},{4,7},{5,4},{6,5},{7,6},{8,11},{9,8},{10,9... | collective-permute-start | bytes 294920 | tf_op jit(solution)/shard_map/ppermute | solution.py:13
  35.4 6.5 %collective-permute-start.7 = (f32[4,4,1536]{2,1,0:T(4,128)S(1)}, f32[4,4,1536]{2,1,0:T(4,128)S(1)}, u32[]{:S(2)}, u32[]{:S(2)}) collective-permute-start(f32[4,4,1536]{2,1,0:T(4,128)S(1)} %get-tuple-element.7), channel_id=1, source_target_pairs={{0,2},{1,3},{2,0},{3,1},{4,6},{5,7},{6,4},{7,5},{8,10},{9,11},{10,... | collective-permute-start | bytes 294920 | tf_op jit(solution)/shard_map/ppermute | solution.py:13
  42.0 6.6 %collective-permute-start.12 = (bf16[4,3072]{1,0:T(4,128)(2,1)S(1)}, bf16[4,3072]{1,0:T(4,128)(2,1)S(1)}, u32[]{:S(2)}, u32[]{:S(2)}) collective-permute-start(bf16[4,3072]{1,0:T(4,128)(2,1)S(1)} %get-tuple-element.29), channel_id=1, source_target_pairs={{0,12},{4,0},{8,4},{12,8},{1,13},{5,1},{9,5},{13,9},{2,14},{6,2},{... | collective-permute-start | bytes 73736 | tf_op jit(solution)/shard_map/ppermute | solution.py:13
  44.9 5.7 %collective-permute-start.14 = (bf16[4,3072]{1,0:T(4,128)(2,1)S(1)}, bf16[4,3072]{1,0:T(4,128)(2,1)S(1)}, u32[]{:S(2)}, u32[]{:S(2)}) collective-permute-start(bf16[4,3072]{1,0:T(4,128)(2,1)S(1)} %get-tuple-element.30), channel_id=1, source_target_pairs={{0,4},{4,8},{8,12},{12,0},{1,5},{5,9},{9,13},{13,1},{2,6},{6,10},{... | collective-permute-start | bytes 73736 | tf_op jit(solution)/shard_map/ppermute | solution.py:13
  44.9 5.7 %collective-permute-start.13 = (bf16[4,3072]{1,0:T(4,128)(2,1)S(1)}, bf16[4,3072]{1,0:T(4,128)(2,1)S(1)}, u32[]{:S(2)}, u32[]{:S(2)}) collective-permute-start(bf16[4,3072]{1,0:T(4,128)(2,1)S(1)} %get-tuple-element.31), channel_id=1, source_target_pairs={{0,8},{4,12},{8,0},{12,4},{1,9},{5,13},{9,1},{13,5},{2,10},{6,14},... | collective-permute-start | bytes 73736 | tf_op jit(solution)/shard_map/ppermute | solution.py:13
  54.1 4.7 %collective-permute-start.17 = (bf16[4,3072]{1,0:T(4,128)(2,1)S(1)}, bf16[4,3072]{1,0:T(4,128)(2,1)S(1)}, u32[]{:S(2)}, u32[]{:S(2)}) collective-permute-start(bf16[4,3072]{1,0:T(4,128)(2,1)S(1)} %get-tuple-element.25), channel_id=1, source_target_pairs={{0,12},{4,0},{8,4},{12,8},{1,13},{5,1},{9,5},{13,9},{2,14},{6,2},{... | collective-permute-start | bytes 73736 | tf_op jit(solution)/shard_map/ppermute | solution.py:13
  57.0 4.7 %collective-permute-start.16 = (bf16[4,3072]{1,0:T(4,128)(2,1)S(1)}, bf16[4,3072]{1,0:T(4,128)(2,1)S(1)}, u32[]{:S(2)}, u32[]{:S(2)}) collective-permute-start(bf16[4,3072]{1,0:T(4,128)(2,1)S(1)} %get-tuple-element.26), channel_id=1, source_target_pairs={{0,8},{4,12},{8,0},{12,4},{1,9},{5,13},{9,1},{13,5},{2,10},{6,14},... | collective-permute-start | bytes 73736 | tf_op jit(solution)/shard_map/ppermute | solution.py:13
  57.0 5.6 %collective-permute-start.15 = (bf16[4,3072]{1,0:T(4,128)(2,1)S(1)}, bf16[4,3072]{1,0:T(4,128)(2,1)S(1)}, u32[]{:S(2)}, u32[]{:S(2)}) collective-permute-start(bf16[4,3072]{1,0:T(4,128)(2,1)S(1)} %get-tuple-element.27), channel_id=1, source_target_pairs={{0,4},{4,8},{8,12},{12,0},{1,5},{5,9},{9,13},{13,1},{2,6},{6,10},{... | collective-permute-start | bytes 73736 | tf_op jit(solution)/shard_map/ppermute | solution.py:13
  62.8 5.0 %collective-permute-start.19 = (bf16[4,4,3072]{2,1,0:T(4,128)(2,1)S(1)}, bf16[4,4,3072]{2,1,0:T(4,128)(2,1)S(1)}, u32[]{:S(2)}, u32[]{:S(2)}) collective-permute-start(bf16[4,4,3072]{2,1,0:T(4,128)(2,1)S(1)} %pad_maximum_fusion.3), channel_id=1, source_target_pairs={{0,2},{1,3},{2,0},{3,1},{4,6},{5,7},{6,4},{7,5},{8,10},{9,11},{10,... | collective-permute-start | bytes 294920 | tf_op jit(solution)/shard_map/ppermute | solution.py:13
  64.2 4.7 %collective-permute-start.18 = (bf16[4,4,3072]{2,1,0:T(4,128)(2,1)S(1)}, bf16[4,4,3072]{2,1,0:T(4,128)(2,1)S(1)}, u32[]{:S(2)}, u32[]{:S(2)}) collective-permute-start(bf16[4,4,3072]{2,1,0:T(4,128)(2,1)S(1)} %pad_maximum_fusion.3), channel_id=1, source_target_pairs={{0,1},{1,2},{2,3},{3,0},{4,5},{5,6},{6,7},{7,4},{8,9},{9,10},{10,1... | collective-permute-start | bytes 294920 | tf_op jit(solution)/shard_map/ppermute | solution.py:13
  64.2 4.7 %collective-permute-start.20 = (bf16[4,4,3072]{2,1,0:T(4,128)(2,1)S(1)}, bf16[4,4,3072]{2,1,0:T(4,128)(2,1)S(1)}, u32[]{:S(2)}, u32[]{:S(2)}) collective-permute-start(bf16[4,4,3072]{2,1,0:T(4,128)(2,1)S(1)} %pad_maximum_fusion.3), channel_id=1, source_target_pairs={{0,3},{1,0},{2,1},{3,2},{4,7},{5,4},{6,5},{7,6},{8,11},{9,8},{10,9... | collective-permute-start | bytes 294920 | tf_op jit(solution)/shard_map/ppermute | solution.py:13
  85.0 18.1 %copy-start.1 = (bf16[4,1024,256]{2,1,0:T(8,128)(2,1)S(1)}, bf16[4,1024,256]{2,1,0:T(8,128)(2,1)}, u32[]{:S(2)}) copy-start(bf16[4,1024,256]{2,1,0:T(8,128)(2,1)} %param.9) | copy-start | bytes 6291460
  85.0 5.4 %collective-permute-start.27 = (bf16[16,1536]{1,0:T(8,128)(2,1)S(1)}, bf16[16,1536]{1,0:T(8,128)(2,1)S(1)}, u32[]{:S(2)}, u32[]{:S(2)}) collective-permute-start(bf16[16,1536]{1,0:T(8,128)(2,1)S(1)} %get-tuple-element.17), channel_id=1, source_target_pairs={{0,12},{4,0},{8,4},{12,8},{1,13},{5,1},{9,5},{13,9},{2,14},{6,2},{... | collective-permute-start | bytes 147464 | tf_op jit(solution)/shard_map/ppermute | solution.py:13
  85.9 6.4 %collective-permute-start.29 = (bf16[16,1536]{1,0:T(8,128)(2,1)S(1)}, bf16[16,1536]{1,0:T(8,128)(2,1)S(1)}, u32[]{:S(2)}, u32[]{:S(2)}) collective-permute-start(bf16[16,1536]{1,0:T(8,128)(2,1)S(1)} %get-tuple-element.18), channel_id=1, source_target_pairs={{0,4},{4,8},{8,12},{12,0},{1,5},{5,9},{9,13},{13,1},{2,6},{6,10},{... | collective-permute-start | bytes 147464 | tf_op jit(solution)/shard_map/ppermute | solution.py:13
  87.1 7.8 %collective-permute-start.28 = (bf16[16,1536]{1,0:T(8,128)(2,1)S(1)}, bf16[16,1536]{1,0:T(8,128)(2,1)S(1)}, u32[]{:S(2)}, u32[]{:S(2)}) collective-permute-start(bf16[16,1536]{1,0:T(8,128)(2,1)S(1)} %get-tuple-element.19), channel_id=1, source_target_pairs={{0,8},{4,12},{8,0},{12,4},{1,9},{5,13},{9,1},{13,5},{2,10},{6,14},... | collective-permute-start | bytes 147464 | tf_op jit(solution)/shard_map/ppermute | solution.py:13
  88.3 6.6 %collective-permute-start.21 = (bf16[16,1536]{1,0:T(8,128)(2,1)S(1)}, bf16[16,1536]{1,0:T(8,128)(2,1)S(1)}, u32[]{:S(2)}, u32[]{:S(2)}) collective-permute-start(bf16[16,1536]{1,0:T(8,128)(2,1)S(1)} %get-tuple-element.11), channel_id=1, source_target_pairs={{0,12},{4,0},{8,4},{12,8},{1,13},{5,1},{9,5},{13,9},{2,14},{6,2},{... | collective-permute-start | bytes 147464 | tf_op jit(solution)/shard_map/ppermute | solution.py:13
  89.8 7.6 %collective-permute-start.23 = (bf16[16,1536]{1,0:T(8,128)(2,1)S(1)}, bf16[16,1536]{1,0:T(8,128)(2,1)S(1)}, u32[]{:S(2)}, u32[]{:S(2)}) collective-permute-start(bf16[16,1536]{1,0:T(8,128)(2,1)S(1)} %get-tuple-element.12), channel_id=1, source_target_pairs={{0,4},{4,8},{8,12},{12,0},{1,5},{5,9},{9,13},{13,1},{2,6},{6,10},{... | collective-permute-start | bytes 147464 | tf_op jit(solution)/shard_map/ppermute | solution.py:13
  90.5 7.5 %collective-permute-start.22 = (bf16[16,1536]{1,0:T(8,128)(2,1)S(1)}, bf16[16,1536]{1,0:T(8,128)(2,1)S(1)}, u32[]{:S(2)}, u32[]{:S(2)}) collective-permute-start(bf16[16,1536]{1,0:T(8,128)(2,1)S(1)} %get-tuple-element.13), channel_id=1, source_target_pairs={{0,8},{4,12},{8,0},{12,4},{1,9},{5,13},{9,1},{13,5},{2,10},{6,14},... | collective-permute-start | bytes 147464 | tf_op jit(solution)/shard_map/ppermute | solution.py:13
  92.3 5.7 %collective-permute-start.24 = (bf16[16,1536]{1,0:T(8,128)(2,1)S(1)}, bf16[16,1536]{1,0:T(8,128)(2,1)S(1)}, u32[]{:S(2)}, u32[]{:S(2)}) collective-permute-start(bf16[16,1536]{1,0:T(8,128)(2,1)S(1)} %get-tuple-element.14), channel_id=1, source_target_pairs={{0,12},{4,0},{8,4},{12,8},{1,13},{5,1},{9,5},{13,9},{2,14},{6,2},{... | collective-permute-start | bytes 147464 | tf_op jit(solution)/shard_map/ppermute | solution.py:13
  94.9 6.1 %collective-permute-start.26 = (bf16[16,1536]{1,0:T(8,128)(2,1)S(1)}, bf16[16,1536]{1,0:T(8,128)(2,1)S(1)}, u32[]{:S(2)}, u32[]{:S(2)}) collective-permute-start(bf16[16,1536]{1,0:T(8,128)(2,1)S(1)} %get-tuple-element.15), channel_id=1, source_target_pairs={{0,4},{4,8},{8,12},{12,0},{1,5},{5,9},{9,13},{13,1},{2,6},{6,10},{... | collective-permute-start | bytes 147464 | tf_op jit(solution)/shard_map/ppermute | solution.py:13
  94.9 7.2 %collective-permute-start.25 = (bf16[16,1536]{1,0:T(8,128)(2,1)S(1)}, bf16[16,1536]{1,0:T(8,128)(2,1)S(1)}, u32[]{:S(2)}, u32[]{:S(2)}) collective-permute-start(bf16[16,1536]{1,0:T(8,128)(2,1)S(1)} %get-tuple-element.16), channel_id=1, source_target_pairs={{0,8},{4,12},{8,0},{12,4},{1,9},{5,13},{9,1},{13,5},{2,10},{6,14},... | collective-permute-start | bytes 147464 | tf_op jit(solution)/shard_map/ppermute | solution.py:13
where the time goes:
time: 104 us; the launch traced here: 103 us
  starting transfers between devices  43.8 us (42%)
  Pallas kernels  32.3 us (31%)
  waiting for transfers between devices  19.6 us (19%)
  matrix products  2.84 us (3%)
  local copies, waits for them, and re-layouts  2.55 us (2%)
  other arithmetic  1.54 us (1%)
    ppermute x30, starting transfers between devices, shift(): return lax.ppermute(x, axis, [(i, (i + step) % size) for i in range(size)])  43.8 us
    pallas_call x6, Pallas kernels, product(): pl.pallas_call(kernel, grid=(width // tile,), in_specs=in_specs, out_spec...  32.3 us
    ppermute x30, waiting for transfers between devices, shift(): return lax.ppermute(x, axis, [(i, (i + step) % size) for i in range(size)])  19.6 us
    dot_general x1, matrix products, step(): jnp.einsum('bhl,bld->bhd', probs, cache_values, preferred_element_type=jn...  2.11 us
  transfers between devices with their start and end apart: 30, of which 12 were waited for; matrix products, arithmetic and copies ran while one was open for 0% of the time, Pallas kernels for 7%

commit v1 on v0

--- a/solution.py
+++ b/solution.py
@@ -63,31 +63,26 @@
     return [(i * (width // count), (i + 1) * (width // count)) for i in range(count)]
 
 
-def product(x, w, k, n, base=None):
+def product(x, w, n):
     rows, depth = x.shape
     width = n[1] - n[0]
-    tile = next(t for t in (512, 384, 256, 128) if width % t == 0 and n[0] % t == 0)
+    tile = next(t for t in (256, 128) if width % t == 0 and n[0] % t == 0)
     first = n[0] // tile
-    row = k[0] // depth
 
-    def kernel(x_ref, w_ref, *rest):
-        acc = jnp.dot(x_ref[...], w_ref[...], preferred_element_type=jnp.float32)
-        rest[-1][...] = acc if base is None else acc + rest[0][...]
+    def kernel(x_ref, w_ref, out_ref):
+        out_ref[...] = jnp.dot(x_ref[...], w_ref[...], preferred_element_type=jnp.float32)
 
-    in_specs = [
-        pl.BlockSpec((rows, depth), lambda j: (0, 0)),
-        pl.BlockSpec((depth, tile), lambda j: (row, first + j)),
-    ]
-    if base is not None:
-        in_specs.append(pl.BlockSpec((rows, tile), lambda j: (0, first + j)))
     return pl.pallas_call(
         kernel,
         grid=(width // tile,),
-        in_specs=in_specs,
+        in_specs=[
+            pl.BlockSpec((rows, depth), lambda j: (0, 0)),
+            pl.BlockSpec((depth, tile), lambda j: (0, first + j)),
+        ],
         out_specs=pl.BlockSpec((rows, tile), lambda j: (0, j)),
         out_shape=jax.ShapeDtypeStruct((rows, width), jnp.float32),
         compiler_params=pltpu.CompilerParams(vmem_limit_bytes=40 * 2**20),
-    )(x, w, *(() if base is None else (base,)))
+    )(x, w)
 
 
 def step(hidden_in, w_query, w_out, cache_keys, cache_values, lengths):
@@ -97,16 +92,14 @@
     rows = across * within * local_seqs
     slice_width = w_query.shape[1]
 
-    k0, k1 = parts(hidden_in.shape[1], 2)
-    x0 = gather(hidden_in[:, k0[0]:k0[1]], "gx").reshape(rows, -1)
-    x1 = gather(hidden_in[:, k1[0]:k1[1]], "gx").reshape(rows, -1)
-    base = product(x0, w_query, k0, (0, slice_width))
+    x = gather(hidden_in, "gx").reshape(across, within, local_seqs, -1)
+    x = x.transpose(1, 0, 2, 3).reshape(rows, -1)
     owned = []
     for n in parts(slice_width, 2):
-        part = product(x1, w_query, k1, n, base)
-        part = part.reshape(across, within, local_seqs, -1).transpose(1, 0, 2, 3)
+        part = product(x, w_query, n)
+        part = part.reshape(within, across * local_seqs, -1)
         owned.append(reduce_to(part, "gy").astype(jnp.bfloat16))
-    owned = jnp.concatenate(owned, axis=2)
+    owned = jnp.concatenate(owned, axis=1).reshape(across, local_seqs, slice_width)
     query = swap(owned, "gx", -1).transpose(1, 0, 2).reshape(local_seqs, -1)
 
     head_count = query.shape[1] // head_dim
@@ -124,8 +117,8 @@
     spread = swap(attended.transpose(1, 0, 2), "gx", 1)
     head_rows = gather(spread, "gy").transpose(1, 0, 2, 3).reshape(rows, slice_width)
     outs = []
-    for n in parts(w_out.shape[1], 3):
-        part = product(head_rows, w_out, (0, slice_width), n)
+    for n in parts(w_out.shape[1], 2):
+        part = product(head_rows, w_out, n)
         part = part.reshape(across, within * local_seqs, -1)
         outs.append(reduce_back(part, "gx", jnp.bfloat16).astype(jnp.bfloat16))
     out = jnp.concatenate(outs, axis=1).reshape(within, local_seqs, -1)

time: 104 us -> 107 us (1.029)
  waiting for transfers between devices: 19.6 us -> 33.6 us
  starting transfers between devices: 43.8 us -> 31.4 us
  Pallas kernels: 32.3 us -> 34.1 us
    ppermute x30 -> x24, waiting for transfers between devices: 19.6 us -> 33.6 us  [shift(): return lax.ppermute(x, axis, [(i, (i + step) % size) for i in range(size)])]
    ppermute x30 -> x24, starting transfers between devices: 43.8 us -> 31.4 us  [shift(): return lax.ppermute(x, axis, [(i, (i + step) % size) for i in range(size)])]
    pallas_call x6 -> x4, Pallas kernels: 32.3 us -> 34.1 us  [product(): pl.pallas_call(kernel, grid=(width // tile,), in_specs=[pl.BlockSpec((row...]
  transfers between devices with their start and end apart: 30 -> 24, of which waited for: 12 -> 18; matrix products, arithmetic and copies ran while one was open for 0% -> 1% of each run, Pallas kernels for 7% -> 0%
where the time goes in v1:
time: 107 us
  Pallas kernels  34.1 us (32%)
  waiting for transfers between devices  33.6 us (31%)
  starting transfers between devices  31.4 us (29%)
  matrix products  2.89 us (3%)
  local copies, waits for them, and re-layouts  2.47 us (2%)
  other arithmetic  1.91 us (2%)
    pallas_call x4, Pallas kernels, product(): pl.pallas_call(kernel, grid=(width // tile,), in_specs=[pl.BlockSpec((row...  34.1 us
    ppermute x24, waiting for transfers between devices, shift(): return lax.ppermute(x, axis, [(i, (i + step) % size) for i in range(size)])  33.6 us
    ppermute x24, starting transfers between devices, shift(): return lax.ppermute(x, axis, [(i, (i + step) % size) for i in range(size)])  31.4 us
    dot_general x1, matrix products, step(): jnp.einsum('bhl,bld->bhd', probs, cache_values, preferred_element_type=jn...  2.15 us
  transfers between devices with their start and end apart: 24, of which 18 were waited for; matrix products, arithmetic and copies ran while one was open for 1% of the time, Pallas kernels for 0%

profile of v1, /device:TPU:0, one launch (start us, length us, event | category | flops | bytes accessed | tf_op | source)
XLA Modules:
  0.0 106.7 jit_solution(11501996658761528970)
XLA Ops:
  0.0 3.1 %collective-permute-start = (bf16[16,4608]{1,0:T(8,128)(2,1)}, bf16[16,4608]{1,0:T(8,128)(2,1)S(1)}, u32[]{:S(2)}, u32[]{:S(2)}) collective-permute-start(bf16[16,4608]{1,0:T(8,128)(2,1)} %param.6), channel_id=1, source_target_pairs={{0,4},{4,8},{8,12},{12,0},{1,5},{5,9},{9,13},{13,1},{2,6},{6,10},{... | collective-permute-start | bytes 442376 | tf_op jit(solution)/shard_map/ppermute | solution.py:13
  3.1 2.6 %collective-permute-start.1 = (bf16[16,4608]{1,0:T(8,128)(2,1)}, bf16[16,4608]{1,0:T(8,128)(2,1)S(1)}, u32[]{:S(2)}, u32[]{:S(2)}) collective-permute-start(bf16[16,4608]{1,0:T(8,128)(2,1)} %param.6), channel_id=1, source_target_pairs={{0,8},{4,12},{8,0},{12,4},{1,9},{5,13},{9,1},{13,5},{2,10},{6,14},... | collective-permute-start | bytes 442376 | tf_op jit(solution)/shard_map/ppermute | solution.py:13
  5.6 1.3 %collective-permute-start.2 = (bf16[16,4608]{1,0:T(8,128)(2,1)}, bf16[16,4608]{1,0:T(8,128)(2,1)S(1)}, u32[]{:S(2)}, u32[]{:S(2)}) collective-permute-start(bf16[16,4608]{1,0:T(8,128)(2,1)} %param.6), channel_id=1, source_target_pairs={{0,12},{4,0},{8,4},{12,8},{1,13},{5,1},{9,5},{13,9},{2,14},{6,2},{... | collective-permute-start | bytes 442376 | tf_op jit(solution)/shard_map/ppermute | solution.py:13
  7.0 1.0 stack.54
  8.0 2.1 %collective-permute-done = bf16[16,4608]{1,0:T(8,128)(2,1)S(1)} collective-permute-done((bf16[16,4608]{1,0:T(8,128)(2,1)}, bf16[16,4608]{1,0:T(8,128)(2,1)S(1)}, u32[]{:S(2)}, u32[]{:S(2)}) %collective-permute-start) | collective-permute-done | bytes 147488 | tf_op jit(solution)/shard_map/ppermute | solution.py:13
  10.1 5.4 %collective-permute-done.1 = bf16[16,4608]{1,0:T(8,128)(2,1)S(1)} collective-permute-done((bf16[16,4608]{1,0:T(8,128)(2,1)}, bf16[16,4608]{1,0:T(8,128)(2,1)S(1)}, u32[]{:S(2)}, u32[]{:S(2)}) %collective-permute-start.1) | collective-permute-done | bytes 147488 | tf_op jit(solution)/shard_map/ppermute | solution.py:13
  15.6 0.5 maximum_bitcast_fusion
  16.3 7.8 %shard_map.65 = f32[64,1536]{1,0:T(8,128)S(1)} custom-call(bf16[64,4608]{1,0:T(8,128)(2,1)S(1)} %reshape.79.x_ref, bf16[4608,3072]{1,0:T(8,128)(2,1)} %w_ref.5), custom_call_target="tpu_custom_call" | custom-call | tf_op jit(solution)/shard_map/pallas_call | solution.py:75
  24.1 7.7 %shard_map.64 = f32[64,1536]{1,0:T(8,128)S(1)} custom-call(bf16[64,4608]{1,0:T(8,128)(2,1)S(1)} %reshape.79.x_ref, bf16[4608,3072]{1,0:T(8,128)(2,1)} %w_ref.5), custom_call_target="tpu_custom_call" | custom-call | tf_op jit(solution)/shard_map/pallas_call | solution.py:75
  31.9 1.6 %collective-permute-start.7 = (f32[16,1536]{1,0:T(8,128)S(1)}, f32[16,1536]{1,0:T(8,128)S(1)}, u32[]{:S(2)}, u32[]{:S(2)}) collective-permute-start(f32[16,1536]{1,0:T(8,128)S(1)} %get-tuple-element.10), channel_id=1, source_target_pairs={{0,2},{1,3},{2,0},{3,1},{4,6},{5,7},{6,4},{7,5},{8,10},{9,11},{10,... | collective-permute-start | bytes 294920 | tf_op jit(solution)/shard_map/ppermute | solution.py:13
  33.5 1.4 %collective-permute-start.8 = (f32[16,1536]{1,0:T(8,128)S(1)}, f32[16,1536]{1,0:T(8,128)S(1)}, u32[]{:S(2)}, u32[]{:S(2)}) collective-permute-start(f32[16,1536]{1,0:T(8,128)S(1)} %get-tuple-element.9), channel_id=1, source_target_pairs={{0,3},{1,0},{2,1},{3,2},{4,7},{5,4},{6,5},{7,6},{8,11},{9,8},{10,9... | collective-permute-start | bytes 294920 | tf_op jit(solution)/shard_map/ppermute | solution.py:13
  34.9 0.6 collective-permute-start.4
  35.5 0.8 collective-permute-done.6
  36.3 0.6 collective-permute-start.5
  36.9 0.7 collective-permute-done.7
  37.6 1.1 %collective-permute-done.8 = f32[16,1536]{1,0:T(8,128)S(1)} collective-permute-done((f32[16,1536]{1,0:T(8,128)S(1)}, f32[16,1536]{1,0:T(8,128)S(1)}, u32[]{:S(2)}, u32[]{:S(2)}) %collective-permute-start.8) | collective-permute-done | bytes 98336 | tf_op jit(solution)/shard_map/ppermute | solution.py:13
  38.8 1.8 %collective-permute-done.3 = f32[16,1536]{1,0:T(8,128)S(1)} collective-permute-done((f32[16,1536]{1,0:T(8,128)S(1)}, f32[16,1536]{1,0:T(8,128)S(1)}, u32[]{:S(2)}, u32[]{:S(2)}) %collective-permute-start.3) | collective-permute-done | bytes 98336 | tf_op jit(solution)/shard_map/ppermute | solution.py:13
  40.5 1.3 %collective-permute-done.4 = f32[16,1536]{1,0:T(8,128)S(1)} collective-permute-done((f32[16,1536]{1,0:T(8,128)S(1)}, f32[16,1536]{1,0:T(8,128)S(1)}, u32[]{:S(2)}, u32[]{:S(2)}) %collective-permute-start.4) | collective-permute-done | bytes 98336 | tf_op jit(solution)/shard_map/ppermute | solution.py:13
  41.9 0.5 collective-permute-done.5
  42.4 4.7 %collective-permute-start.9 = (bf16[4,3072]{1,0:T(4,128)(2,1)S(1)}, bf16[4,3072]{1,0:T(4,128)(2,1)S(1)}, u32[]{:S(2)}, u32[]{:S(2)}) collective-permute-start(bf16[4,3072]{1,0:T(4,128)(2,1)S(1)} %get-tuple-element.22), channel_id=1, source_target_pairs={{0,12},{4,0},{8,4},{12,8},{1,13},{5,1},{9,5},{13,9},{2,14},{6,2},{... | collective-permute-start | bytes 73736 | tf_op jit(solution)/shard_map/ppermute | solution.py:13
  47.1 0.3 collective-permute-start.10
  47.5 0.3 collective-permute-start.11
  47.9 0.9 collective-permute-done.9
  48.7 3.1 %collective-permute-done.10 = bf16[4,3072]{1,0:T(4,128)(2,1)S(1)} collective-permute-done((bf16[4,3072]{1,0:T(4,128)(2,1)S(1)}, bf16[4,3072]{1,0:T(4,128)(2,1)S(1)}, u32[]{:S(2)}, u32[]{:S(2)}) %collective-permute-start.10) | collective-permute-done | bytes 24608 | tf_op jit(solution)/shard_map/ppermute | solution.py:13
  51.9 1.2 %collective-permute-done.11 = bf16[4,3072]{1,0:T(4,128)(2,1)S(1)} collective-permute-done((bf16[4,3072]{1,0:T(4,128)(2,1)S(1)}, bf16[4,3072]{1,0:T(4,128)(2,1)S(1)}, u32[]{:S(2)}, u32[]{:S(2)}) %collective-permute-start.11) | collective-permute-done | bytes 24608 | tf_op jit(solution)/shard_map/ppermute | solution.py:13
  53.3 0.7 fusion.4
  54.1 0.3 fusion.28
  54.4 2.1 %convolution_convert_fusion = bf16[4,48,256]{2,1,0:T(8,128)(2,1)S(1)} fusion(bf16[4,1024,256]{2,1,0:T(8,128)(2,1)} %param.10, f32[4,48]{1,0:T(4,128)S(1)} %fusion.28, f32[4,48,1024]{2,1,0:T(8,128)S(1)} %fusion.4, pred[4,1024]{1,0:T(4,128)(4,1)S(1)} %iota_compare_fusion), kind=kOutput, calls=%fused_computation.6 | convolution fusion | flops 101500096 | bytes 2986752 | tf_op jit(solution)/shard_map/bhl,bld->bhd/dot_general | solution.py:114
  56.8 0.8 collective-permute-start.13
  57.6 3.0 %collective-permute-start.14 = (bf16[4,3072]{1,0:T(4,128)(2,1)S(1)}, bf16[4,3072]{1,0:T(4,128)(2,1)S(1)}, u32[]{:S(2)}, u32[]{:S(2)}) collective-permute-start(bf16[4,3072]{1,0:T(4,128)(2,1)S(1)} %get-tuple-element.18), channel_id=1, source_target_pairs={{0,12},{4,0},{8,4},{12,8},{1,13},{5,1},{9,5},{13,9},{2,14},{6,2},{... | collective-permute-start | bytes 73736 | tf_op jit(solution)/shard_map/ppermute | solution.py:13
  60.6 1.8 %collective-permute-done.12 = bf16[4,3072]{1,0:T(4,128)(2,1)S(1)} collective-permute-done((bf16[4,3072]{1,0:T(4,128)(2,1)S(1)}, bf16[4,3072]{1,0:T(4,128)(2,1)S(1)}, u32[]{:S(2)}, u32[]{:S(2)}) %collective-permute-start.12) | collective-permute-done | bytes 24608 | tf_op jit(solution)/shard_map/ppermute | solution.py:13
  62.4 0.6 collective-permute-done.14
  63.1 1.1 %collective-permute-start.16 = (bf16[4,4,3072]{2,1,0:T(4,128)(2,1)S(1)}, bf16[4,4,3072]{2,1,0:T(4,128)(2,1)S(1)}, u32[]{:S(2)}, u32[]{:S(2)}) collective-permute-start(bf16[4,4,3072]{2,1,0:T(4,128)(2,1)S(1)} %pad_maximum_fusion.1), channel_id=1, source_target_pairs={{0,2},{1,3},{2,0},{3,1},{4,6},{5,7},{6,4},{7,5},{8,10},{9,11},{10,... | collective-permute-start | bytes 294920 | tf_op jit(solution)/shard_map/ppermute | solution.py:13
  64.2 1.4 %collective-permute-start.17 = (bf16[4,4,3072]{2,1,0:T(4,128)(2,1)S(1)}, bf16[4,4,3072]{2,1,0:T(4,128)(2,1)S(1)}, u32[]{:S(2)}, u32[]{:S(2)}) collective-permute-start(bf16[4,4,3072]{2,1,0:T(4,128)(2,1)S(1)} %pad_maximum_fusion.1), channel_id=1, source_target_pairs={{0,3},{1,0},{2,1},{3,2},{4,7},{5,4},{6,5},{7,6},{8,11},{9,8},{10,9... | collective-permute-start | bytes 294920 | tf_op jit(solution)/shard_map/ppermute | solution.py:13
  65.7 1.8 %collective-permute-done.15 = bf16[4,4,3072]{2,1,0:T(4,128)(2,1)S(1)} collective-permute-done((bf16[4,4,3072]{2,1,0:T(4,128)(2,1)S(1)}, bf16[4,4,3072]{2,1,0:T(4,128)(2,1)S(1)}, u32[]{:S(2)}, u32[]{:S(2)}) %collective-permute-start.15) | collective-permute-done | bytes 98336 | tf_op jit(solution)/shard_map/ppermute | solution.py:13
  67.5 1.3 %collective-permute-done.16 = bf16[4,4,3072]{2,1,0:T(4,128)(2,1)S(1)} collective-permute-done((bf16[4,4,3072]{2,1,0:T(4,128)(2,1)S(1)}, bf16[4,4,3072]{2,1,0:T(4,128)(2,1)S(1)}, u32[]{:S(2)}, u32[]{:S(2)}) %collective-permute-start.16) | collective-permute-done | bytes 98336 | tf_op jit(solution)/shard_map/ppermute | solution.py:13
  68.9 0.3 maximum_bitcast_fusion.1
  69.3 9.3 %shard_map.66 = f32[64,2304]{1,0:T(8,128)S(1)} custom-call(bf16[64,3072]{1,0:T(8,128)(2,1)S(1)} %reshape.83.x_ref, bf16[3072,4608]{1,0:T(8,128)(2,1)} %w_ref.7), custom_call_target="tpu_custom_call" | custom-call | tf_op jit(solution)/shard_map/pallas_call | solution.py:75
  78.5 9.3 %shard_map.67 = f32[64,2304]{1,0:T(8,128)S(1)} custom-call(bf16[64,3072]{1,0:T(8,128)(2,1)S(1)} %reshape.83.x_ref, bf16[3072,4608]{1,0:T(8,128)(2,1)} %w_ref.7), custom_call_target="tpu_custom_call" | custom-call | tf_op jit(solution)/shard_map/pallas_call | solution.py:75
  87.9 3.3 %collective-permute-start.18 = (bf16[16,2304]{1,0:T(8,128)(2,1)S(1)}, bf16[16,2304]{1,0:T(8,128)(2,1)S(1)}, u32[]{:S(2)}, u32[]{:S(2)}) collective-permute-start(bf16[16,2304]{1,0:T(8,128)(2,1)S(1)} %get-tuple-element.11), channel_id=1, source_target_pairs={{0,12},{4,0},{8,4},{12,8},{1,13},{5,1},{9,5},{13,9},{2,14},{6,2},{... | collective-permute-start | bytes 221192 | tf_op jit(solution)/shard_map/ppermute | solution.py:13
  91.2 0.2 collective-permute-start.19
  91.5 0.4 collective-permute-start.20
  91.9 3.5 %collective-permute-start.21 = (bf16[16,2304]{1,0:T(8,128)(2,1)S(1)}, bf16[16,2304]{1,0:T(8,128)(2,1)S(1)}, u32[]{:S(2)}, u32[]{:S(2)}) collective-permute-start(bf16[16,2304]{1,0:T(8,128)(2,1)S(1)} %get-tuple-element.14), channel_id=1, source_target_pairs={{0,12},{4,0},{8,4},{12,8},{1,13},{5,1},{9,5},{13,9},{2,14},{6,2},{... | collective-permute-start | bytes 221192 | tf_op jit(solution)/shard_map/ppermute | solution.py:13
  95.4 0.9 collective-permute-start.22
  96.3 3.0 %collective-permute-done.19 = bf16[16,2304]{1,0:T(8,128)(2,1)S(1)} collective-permute-done((bf16[16,2304]{1,0:T(8,128)(2,1)S(1)}, bf16[16,2304]{1,0:T(8,128)(2,1)S(1)}, u32[]{:S(2)}, u32[]{:S(2)}) %collective-permute-start.19) | collective-permute-done | bytes 73760 | tf_op jit(solution)/shard_map/ppermute | solution.py:13
  99.3 1.5 %collective-permute-done.21 = bf16[16,2304]{1,0:T(8,128)(2,1)S(1)} collective-permute-done((bf16[16,2304]{1,0:T(8,128)(2,1)S(1)}, bf16[16,2304]{1,0:T(8,128)(2,1)S(1)}, u32[]{:S(2)}, u32[]{:S(2)}) %collective-permute-start.21) | collective-permute-done | bytes 73760 | tf_op jit(solution)/shard_map/ppermute | solution.py:13
  100.8 4.7 %collective-permute-done.22 = bf16[16,2304]{1,0:T(8,128)(2,1)S(1)} collective-permute-done((bf16[16,2304]{1,0:T(8,128)(2,1)S(1)}, bf16[16,2304]{1,0:T(8,128)(2,1)S(1)}, u32[]{:S(2)}, u32[]{:S(2)}) %collective-permute-start.22) | collective-permute-done | bytes 73760 | tf_op jit(solution)/shard_map/ppermute | solution.py:13
  105.9 0.7 reshape.85
  (46 shorter events, 1.8 us)
Async XLA Ops:
  0.0 53.3 %copy-start = (bf16[4,1024,256]{2,1,0:T(8,128)(2,1)S(1)}, bf16[4,1024,256]{2,1,0:T(8,128)(2,1)}, u32[]{:S(2)}) copy-start(bf16[4,1024,256]{2,1,0:T(8,128)(2,1)} %param.9) | copy-start | bytes 6291460
  0.0 10.1 %collective-permute-start = (bf16[16,4608]{1,0:T(8,128)(2,1)}, bf16[16,4608]{1,0:T(8,128)(2,1)S(1)}, u32[]{:S(2)}, u32[]{:S(2)}) collective-permute-start(bf16[16,4608]{1,0:T(8,128)(2,1)} %param.6), channel_id=1, source_target_pairs={{0,4},{4,8},{8,12},{12,0},{1,5},{5,9},{9,13},{13,1},{2,6},{6,10},{... | collective-permute-start | bytes 442376 | tf_op jit(solution)/shard_map/ppermute | solution.py:13
  3.1 12.5 %collective-permute-start.1 = (bf16[16,4608]{1,0:T(8,128)(2,1)}, bf16[16,4608]{1,0:T(8,128)(2,1)S(1)}, u32[]{:S(2)}, u32[]{:S(2)}) collective-permute-start(bf16[16,4608]{1,0:T(8,128)(2,1)} %param.6), channel_id=1, source_target_pairs={{0,8},{4,12},{8,0},{12,4},{1,9},{5,13},{9,1},{13,5},{2,10},{6,14},... | collective-permute-start | bytes 442376 | tf_op jit(solution)/shard_map/ppermute | solution.py:13
  5.6 9.9 %collective-permute-start.2 = (bf16[16,4608]{1,0:T(8,128)(2,1)}, bf16[16,4608]{1,0:T(8,128)(2,1)S(1)}, u32[]{:S(2)}, u32[]{:S(2)}) collective-permute-start(bf16[16,4608]{1,0:T(8,128)(2,1)} %param.6), channel_id=1, source_target_pairs={{0,12},{4,0},{8,4},{12,8},{1,13},{5,1},{9,5},{13,9},{2,14},{6,2},{... | collective-permute-start | bytes 442376 | tf_op jit(solution)/shard_map/ppermute | solution.py:13
  31.8 16.0 %copy-start.2 = (s32[4]{0:T(128)S(1)}, s32[4]{0:T(128)}, u32[]{:S(2)}) copy-start(s32[4]{0:T(128)} %param.11) | copy-start | bytes 52
  31.8 4.5 %collective-permute-start.6 = (f32[16,1536]{1,0:T(8,128)S(1)}, f32[16,1536]{1,0:T(8,128)S(1)}, u32[]{:S(2)}, u32[]{:S(2)}) collective-permute-start(f32[16,1536]{1,0:T(8,128)S(1)} %get-tuple-element.8), channel_id=1, source_target_pairs={{0,1},{1,2},{2,3},{3,0},{4,5},{5,6},{6,7},{7,4},{8,9},{9,10},{10,1... | collective-permute-start | bytes 294920 | tf_op jit(solution)/shard_map/ppermute | solution.py:13
  31.9 5.7 %collective-permute-start.7 = (f32[16,1536]{1,0:T(8,128)S(1)}, f32[16,1536]{1,0:T(8,128)S(1)}, u32[]{:S(2)}, u32[]{:S(2)}) collective-permute-start(f32[16,1536]{1,0:T(8,128)S(1)} %get-tuple-element.10), channel_id=1, source_target_pairs={{0,2},{1,3},{2,0},{3,1},{4,6},{5,7},{6,4},{7,5},{8,10},{9,11},{10,... | collective-permute-start | bytes 294920 | tf_op jit(solution)/shard_map/ppermute | solution.py:13
  33.5 5.3 %collective-permute-start.8 = (f32[16,1536]{1,0:T(8,128)S(1)}, f32[16,1536]{1,0:T(8,128)S(1)}, u32[]{:S(2)}, u32[]{:S(2)}) collective-permute-start(f32[16,1536]{1,0:T(8,128)S(1)} %get-tuple-element.9), channel_id=1, source_target_pairs={{0,3},{1,0},{2,1},{3,2},{4,7},{5,4},{6,5},{7,6},{8,11},{9,8},{10,9... | collective-permute-start | bytes 294920 | tf_op jit(solution)/shard_map/ppermute | solution.py:13
  34.9 5.7 %collective-permute-start.3 = (f32[16,1536]{1,0:T(8,128)S(1)}, f32[16,1536]{1,0:T(8,128)S(1)}, u32[]{:S(2)}, u32[]{:S(2)}) collective-permute-start(f32[16,1536]{1,0:T(8,128)S(1)} %get-tuple-element.5), channel_id=1, source_target_pairs={{0,1},{1,2},{2,3},{3,0},{4,5},{5,6},{6,7},{7,4},{8,9},{9,10},{10,1... | collective-permute-start | bytes 294920 | tf_op jit(solution)/shard_map/ppermute | solution.py:13
  34.9 6.9 %collective-permute-start.4 = (f32[16,1536]{1,0:T(8,128)S(1)}, f32[16,1536]{1,0:T(8,128)S(1)}, u32[]{:S(2)}, u32[]{:S(2)}) collective-permute-start(f32[16,1536]{1,0:T(8,128)S(1)} %get-tuple-element.7), channel_id=1, source_target_pairs={{0,2},{1,3},{2,0},{3,1},{4,6},{5,7},{6,4},{7,5},{8,10},{9,11},{10,... | collective-permute-start | bytes 294920 | tf_op jit(solution)/shard_map/ppermute | solution.py:13
  36.3 6.0 %collective-permute-start.5 = (f32[16,1536]{1,0:T(8,128)S(1)}, f32[16,1536]{1,0:T(8,128)S(1)}, u32[]{:S(2)}, u32[]{:S(2)}) collective-permute-start(f32[16,1536]{1,0:T(8,128)S(1)} %get-tuple-element.6), channel_id=1, source_target_pairs={{0,3},{1,0},{2,1},{3,2},{4,7},{5,4},{6,5},{7,6},{8,11},{9,8},{10,9... | collective-permute-start | bytes 294920 | tf_op jit(solution)/shard_map/ppermute | solution.py:13
  42.4 6.4 %collective-permute-start.9 = (bf16[4,3072]{1,0:T(4,128)(2,1)S(1)}, bf16[4,3072]{1,0:T(4,128)(2,1)S(1)}, u32[]{:S(2)}, u32[]{:S(2)}) collective-permute-start(bf16[4,3072]{1,0:T(4,128)(2,1)S(1)} %get-tuple-element.22), channel_id=1, source_target_pairs={{0,12},{4,0},{8,4},{12,8},{1,13},{5,1},{9,5},{13,9},{2,14},{6,2},{... | collective-permute-start | bytes 73736 | tf_op jit(solution)/shard_map/ppermute | solution.py:13
  47.1 4.7 %collective-permute-start.10 = (bf16[4,3072]{1,0:T(4,128)(2,1)S(1)}, bf16[4,3072]{1,0:T(4,128)(2,1)S(1)}, u32[]{:S(2)}, u32[]{:S(2)}) collective-permute-start(bf16[4,3072]{1,0:T(4,128)(2,1)S(1)} %get-tuple-element.24), channel_id=1, source_target_pairs={{0,8},{4,12},{8,0},{12,4},{1,9},{5,13},{9,1},{13,5},{2,10},{6,14},... | collective-permute-start | bytes 73736 | tf_op jit(solution)/shard_map/ppermute | solution.py:13
  47.5 5.6 %collective-permute-start.11 = (bf16[4,3072]{1,0:T(4,128)(2,1)S(1)}, bf16[4,3072]{1,0:T(4,128)(2,1)S(1)}, u32[]{:S(2)}, u32[]{:S(2)}) collective-permute-start(bf16[4,3072]{1,0:T(4,128)(2,1)S(1)} %get-tuple-element.23), channel_id=1, source_target_pairs={{0,4},{4,8},{8,12},{12,0},{1,5},{5,9},{9,13},{13,1},{2,6},{6,10},{... | collective-permute-start | bytes 73736 | tf_op jit(solution)/shard_map/ppermute | solution.py:13
  56.7 5.7 %collective-permute-start.12 = (bf16[4,3072]{1,0:T(4,128)(2,1)S(1)}, bf16[4,3072]{1,0:T(4,128)(2,1)S(1)}, u32[]{:S(2)}, u32[]{:S(2)}) collective-permute-start(bf16[4,3072]{1,0:T(4,128)(2,1)S(1)} %get-tuple-element.20), channel_id=1, source_target_pairs={{0,4},{4,8},{8,12},{12,0},{1,5},{5,9},{9,13},{13,1},{2,6},{6,10},{... | collective-permute-start | bytes 73736 | tf_op jit(solution)/shard_map/ppermute | solution.py:13
  56.8 5.6 %collective-permute-start.13 = (bf16[4,3072]{1,0:T(4,128)(2,1)S(1)}, bf16[4,3072]{1,0:T(4,128)(2,1)S(1)}, u32[]{:S(2)}, u32[]{:S(2)}) collective-permute-start(bf16[4,3072]{1,0:T(4,128)(2,1)S(1)} %get-tuple-element.19), channel_id=1, source_target_pairs={{0,8},{4,12},{8,0},{12,4},{1,9},{5,13},{9,1},{13,5},{2,10},{6,14},... | collective-permute-start | bytes 73736 | tf_op jit(solution)/shard_map/ppermute | solution.py:13
  57.6 5.3 %collective-permute-start.14 = (bf16[4,3072]{1,0:T(4,128)(2,1)S(1)}, bf16[4,3072]{1,0:T(4,128)(2,1)S(1)}, u32[]{:S(2)}, u32[]{:S(2)}) collective-permute-start(bf16[4,3072]{1,0:T(4,128)(2,1)S(1)} %get-tuple-element.18), channel_id=1, source_target_pairs={{0,12},{4,0},{8,4},{12,8},{1,13},{5,1},{9,5},{13,9},{2,14},{6,2},{... | collective-permute-start | bytes 73736 | tf_op jit(solution)/shard_map/ppermute | solution.py:13
  63.1 4.5 %collective-permute-start.15 = (bf16[4,4,3072]{2,1,0:T(4,128)(2,1)S(1)}, bf16[4,4,3072]{2,1,0:T(4,128)(2,1)S(1)}, u32[]{:S(2)}, u32[]{:S(2)}) collective-permute-start(bf16[4,4,3072]{2,1,0:T(4,128)(2,1)S(1)} %pad_maximum_fusion.1), channel_id=1, source_target_pairs={{0,1},{1,2},{2,3},{3,0},{4,5},{5,6},{6,7},{7,4},{8,9},{9,10},{10,1... | collective-permute-start | bytes 294920 | tf_op jit(solution)/shard_map/ppermute | solution.py:13
  63.1 5.7 %collective-permute-start.16 = (bf16[4,4,3072]{2,1,0:T(4,128)(2,1)S(1)}, bf16[4,4,3072]{2,1,0:T(4,128)(2,1)S(1)}, u32[]{:S(2)}, u32[]{:S(2)}) collective-permute-start(bf16[4,4,3072]{2,1,0:T(4,128)(2,1)S(1)} %pad_maximum_fusion.1), channel_id=1, source_target_pairs={{0,2},{1,3},{2,0},{3,1},{4,6},{5,7},{6,4},{7,5},{8,10},{9,11},{10,... | collective-permute-start | bytes 294920 | tf_op jit(solution)/shard_map/ppermute | solution.py:13
  64.2 4.6 %collective-permute-start.17 = (bf16[4,4,3072]{2,1,0:T(4,128)(2,1)S(1)}, bf16[4,4,3072]{2,1,0:T(4,128)(2,1)S(1)}, u32[]{:S(2)}, u32[]{:S(2)}) collective-permute-start(bf16[4,4,3072]{2,1,0:T(4,128)(2,1)S(1)} %pad_maximum_fusion.1), channel_id=1, source_target_pairs={{0,3},{1,0},{2,1},{3,2},{4,7},{5,4},{6,5},{7,6},{8,11},{9,8},{10,9... | collective-permute-start | bytes 294920 | tf_op jit(solution)/shard_map/ppermute | solution.py:13
  87.8 18.8 %copy-start.1 = (bf16[4,1024,256]{2,1,0:T(8,128)(2,1)S(1)}, bf16[4,1024,256]{2,1,0:T(8,128)(2,1)}, u32[]{:S(2)}) copy-start(bf16[4,1024,256]{2,1,0:T(8,128)(2,1)} %param.9) | copy-start | bytes 6291460
  87.9 8.4 %collective-permute-start.18 = (bf16[16,2304]{1,0:T(8,128)(2,1)S(1)}, bf16[16,2304]{1,0:T(8,128)(2,1)S(1)}, u32[]{:S(2)}, u32[]{:S(2)}) collective-permute-start(bf16[16,2304]{1,0:T(8,128)(2,1)S(1)} %get-tuple-element.11), channel_id=1, source_target_pairs={{0,12},{4,0},{8,4},{12,8},{1,13},{5,1},{9,5},{13,9},{2,14},{6,2},{... | collective-permute-start | bytes 221192 | tf_op jit(solution)/shard_map/ppermute | solution.py:13
  91.2 8.1 %collective-permute-start.19 = (bf16[16,2304]{1,0:T(8,128)(2,1)S(1)}, bf16[16,2304]{1,0:T(8,128)(2,1)S(1)}, u32[]{:S(2)}, u32[]{:S(2)}) collective-permute-start(bf16[16,2304]{1,0:T(8,128)(2,1)S(1)} %get-tuple-element.13), channel_id=1, source_target_pairs={{0,8},{4,12},{8,0},{12,4},{1,9},{5,13},{9,1},{13,5},{2,10},{6,14},... | collective-permute-start | bytes 221192 | tf_op jit(solution)/shard_map/ppermute | solution.py:13
  91.5 7.8 %collective-permute-start.20 = (bf16[16,2304]{1,0:T(8,128)(2,1)S(1)}, bf16[16,2304]{1,0:T(8,128)(2,1)S(1)}, u32[]{:S(2)}, u32[]{:S(2)}) collective-permute-start(bf16[16,2304]{1,0:T(8,128)(2,1)S(1)} %get-tuple-element.12), channel_id=1, source_target_pairs={{0,4},{4,8},{8,12},{12,0},{1,5},{5,9},{9,13},{13,1},{2,6},{6,10},{... | collective-permute-start | bytes 221192 | tf_op jit(solution)/shard_map/ppermute | solution.py:13
  91.9 8.9 %collective-permute-start.21 = (bf16[16,2304]{1,0:T(8,128)(2,1)S(1)}, bf16[16,2304]{1,0:T(8,128)(2,1)S(1)}, u32[]{:S(2)}, u32[]{:S(2)}) collective-permute-start(bf16[16,2304]{1,0:T(8,128)(2,1)S(1)} %get-tuple-element.14), channel_id=1, source_target_pairs={{0,12},{4,0},{8,4},{12,8},{1,13},{5,1},{9,5},{13,9},{2,14},{6,2},{... | collective-permute-start | bytes 221192 | tf_op jit(solution)/shard_map/ppermute | solution.py:13
  95.4 10.2 %collective-permute-start.22 = (bf16[16,2304]{1,0:T(8,128)(2,1)S(1)}, bf16[16,2304]{1,0:T(8,128)(2,1)S(1)}, u32[]{:S(2)}, u32[]{:S(2)}) collective-permute-start(bf16[16,2304]{1,0:T(8,128)(2,1)S(1)} %get-tuple-element.16), channel_id=1, source_target_pairs={{0,8},{4,12},{8,0},{12,4},{1,9},{5,13},{9,1},{13,5},{2,10},{6,14},... | collective-permute-start | bytes 221192 | tf_op jit(solution)/shard_map/ppermute | solution.py:13
  96.3 9.3 %collective-permute-start.23 = (bf16[16,2304]{1,0:T(8,128)(2,1)S(1)}, bf16[16,2304]{1,0:T(8,128)(2,1)S(1)}, u32[]{:S(2)}, u32[]{:S(2)}) collective-permute-start(bf16[16,2304]{1,0:T(8,128)(2,1)S(1)} %get-tuple-element.15), channel_id=1, source_target_pairs={{0,4},{4,8},{8,12},{12,0},{1,5},{5,9},{9,13},{13,1},{2,6},{6,10},{... | collective-permute-start | bytes 221192 | tf_op jit(solution)/shard_map/ppermute | solution.py:13
